TPU v7x, 128 devices: a whole 4x4x4 slice. The times are simulated.
128 devices in a mesh: dp: 4 (over z_hi, core), ctx: 32 (over z_lo, y, x).
Axes of the slice: x: 4, y: 4, z: 4 (z_hi: 2, z_lo: 2; z = z_hi * 2 + z_lo), core: 2. Of those that a mesh axis runs over, the one named last changes fastest.
Arguments:
- density: float32 [512, 64, 64], P(('dp', 'ctx')), parts along dimension 0, may hold values from 0.1 to 50, as said below
- stem_weight: bfloat16 [216, 1024], replicated, may hold values from -0.4375 to 0.4375
- stem_bias: float32 [1024], replicated, may hold values from -3 to 3
- pos_embed: bfloat16 [8192, 1024], P('ctx'), may hold values from -3 to 3
- ln1_gain: float32 [1024], replicated, may hold values from 0.25 to 1.75
- ln1_bias: float32 [1024], replicated, may hold values from -2 to 2
- w_qkv: bfloat16 [1024, 3072], replicated, may hold values from -2 to 2
- qkv_bias: float32 [3072], replicated, may hold values from -2 to 2
- w_out: bfloat16 [1024, 1024], replicated, may hold values from -0.1875 to 0.1875
- out_bias: float32 [1024], replicated, may hold values from -2 to 2
- ln2_gain: float32 [1024], replicated, may hold values from 0.25 to 1.75
- ln2_bias: float32 [1024], replicated, may hold values from -2 to 2
- w_fc1: bfloat16 [1024, 4096], replicated, may hold values from -0.1875 to 0.1875
- fc1_bias: float32 [4096], replicated, may hold values from -3 to 3
- w_fc2: bfloat16 [4096, 1024], replicated, may hold values from -0.09375 to 0.09375
- fc2_bias: float32 [1024], replicated, may hold values from -2 to 2
Outputs:
- encoded: bfloat16 [32768, 1024], P(('dp', 'ctx')), parts along dimension 0
There are 4 independent parts, one for each index of `dp`. A program takes and returns all parts, laid end to end along the dimension named above; an argument that names none is the same for every part. Nothing has to cross between parts.
Inputs may be any that keep to these rules, and one draw needn't show every extreme that they name: density is positive.
All inputs are finite; a program needn't handle non-finite values.
Results may differ from a plain program's by a relative error of at most 0.013.
Values may be sent and summed in bfloat16 or wider, within the bound.
A program may use at most 384 MiB of HBM per device.

v0:
```python
import math

import jax
import jax.numpy as jnp
from jax import lax
from jax.experimental import pallas as pl
from jax.experimental.pallas import tpu as pltpu
from jax.sharding import PartitionSpec as P

F32 = jnp.float32
BF16 = jnp.bfloat16
HEADS = 16
HEAD = 64
VROWS = 80
PLANE = 16
ROW = 4
MESH = pl.DeviceIdType.MESH
VMEM_LIMIT = 58 * 2**20


def remote(src, dst, send, recv, index):
    return pltpu.make_async_remote_copy(
        src_ref=src,
        dst_ref=dst,
        send_sem=send,
        recv_sem=recv,
        device_id={"ctx": index},
        device_id_type=MESH,
    )


def greet(peers):
    barrier = pltpu.get_barrier_semaphore()
    for peer in peers:
        pl.semaphore_signal(barrier, inc=1, device_id={"ctx": peer}, device_id_type=MESH)
    return barrier


def normalize(rows, gain, shift):
    center = rows - jnp.mean(rows, axis=-1, keepdims=True)
    spread = jnp.mean(center * center, axis=-1, keepdims=True)
    return center * lax.rsqrt(spread + 1e-06) * gain + shift


def plane_order(me):
    y, x = lax.rem(lax.div(me, ROW), ROW), lax.rem(me, ROW)
    order = []
    for i in (0, 1, 3, 2):
        for j in range(ROW):
            order.append((i, j, lax.rem(y + i, ROW), lax.rem(x + j, ROW)))
    return order


def front(density, stem_weight, stem_bias, pos, gain, shift, w_qkv, qkv_bias, cells):
    planes, side, _ = density.shape
    count = lax.axis_size("ctx")
    width = stem_weight.shape[1]
    tokens = pos.shape[0]
    grid = side // 4
    lanes = grid * 128
    scale = math.log2(math.e) / math.sqrt(HEAD)
    pad = 72

    def kernel(
        d_ref, ws_ref, sb_ref, pos_ref, g_ref, b_ref, wq_ref, qb_ref,
        res_ref, q_ref, kv_ref,
        mine, sums, halo, fp, x6, w6, wq, posv, blocks,
        sum_s, sum_r, halo_s, halo_r, q_s, q_r, kv_s, kv_r, f_s, f_r, load,
    ):
        me = lax.axis_index("ctx")
        half = lax.div(me, PLANE)
        here = lax.rem(me, PLANE)
        peers = [lax.rem(me + i, count) for i in range(1, count)]
        barrier = greet(peers)
        load_w = pltpu.make_async_copy(wq_ref, wq, load.at[0])
        load_w.start()
        load_p = pltpu.make_async_copy(pos_ref, posv, load.at[1])
        load_p.start()

        slab = d_ref[...]
        part = jnp.sum(slab, axis=0)
        part = jnp.sum(part, axis=0, keepdims=True)
        part = jnp.sum(part, axis=1, keepdims=True)
        mine[...] = jnp.broadcast_to(part, (8, 128))
        pl.semaphore_wait(barrier, count - 1)

        up, down = peers[0], peers[-1]
        to_up = remote(d_ref.at[planes - 1], halo.at[0], halo_s.at[0], halo_r.at[0], up)
        to_down = remote(d_ref.at[0], halo.at[1], halo_s.at[1], halo_r.at[1], down)
        to_up.start()
        to_down.start()
        shares = []
        for i, peer in enumerate(peers):
            shares.append(remote(mine, sums.at[i], sum_s.at[i], sum_r.at[i], peer))
            shares[-1].start()

        fp[...] = jnp.zeros(fp.shape, F32)
        w6[...] = jnp.zeros(w6.shape, BF16)
        for a in range(6):
            w6[a * 128 : a * 128 + 36, :] = ws_ref[a * 36 : (a + 1) * 36, :]

        for share in shares:
            share.wait()
        to_up.wait()
        to_down.wait()
        total = mine[...] + jnp.sum(sums[...], axis=0)
        mean = (total / cells)[0:1, 0:1]

        def logged(values):
            return jnp.log(values / mean).astype(BF16).astype(F32)

        low = jnp.where(me > 0, logged(halo[0]), 0.0)
        high = jnp.where(me < count - 1, logged(halo[1]), 0.0)
        own = logged(slab.reshape(planes * side, side))
        fp[1 : 1 + side, 0:side] = low
        for a in range(planes):
            at = (a + 1) * pad + 1
            fp[at : at + side, 0:side] = own[a * side : (a + 1) * side, :]
        at = (planes + 1) * pad + 1
        fp[at : at + side, 0:side] = high

        z = lax.broadcasted_iota(jnp.int32, (side, lanes), 0)
        col = lax.broadcasted_iota(jnp.int32, (side, lanes), 1)
        lane = jnp.bitwise_and(col, 127)
        base = z + 1 - 4 * jnp.right_shift(col, 7) - lane
        spread = jnp.zeros((6 * grid, lanes), F32)
        for b in range(6):
            rows = jnp.concatenate(
                [fp[pl.ds(a * pad + b, grid, stride=4), 0:side] for a in range(6)], axis=0
            )
            pick = (base == -6 * b) & (lane >= 6 * b) & (lane < 6 * b + 6)
            spread += jnp.dot(
                rows.astype(BF16),
                jnp.where(pick, 1.0, 0.0).astype(BF16),
                preferred_element_type=F32,
            )
        spread = spread.astype(BF16)
        for k in range(grid):
            for a in range(6):
                x6[k * grid : (k + 1) * grid, a * 128 : (a + 1) * 128] = spread[
                    a * grid : (a + 1) * grid, k * 128 : (k + 1) * 128
                ]
        r = lax.broadcasted_iota(jnp.int32, (tokens, tokens), 0)
        s = lax.broadcasted_iota(jnp.int32, (tokens, tokens), 1)
        turn = (jnp.right_shift(r, 4) == jnp.bitwise_and(s, 15)) & (
            jnp.bitwise_and(r, 15) == jnp.right_shift(s, 4)
        )
        patches = jnp.dot(
            jnp.where(turn, 1.0, 0.0).astype(BF16), x6[...], preferred_element_type=F32
        ).astype(BF16)
        load_p.wait()
        embedded = (
            jnp.dot(patches, w6[...], preferred_element_type=F32)
            + sb_ref[...]
            + posv[...].astype(F32)
        )
        residual = embedded.astype(BF16)
        res_ref[...] = residual
        normed = normalize(residual.astype(F32), g_ref[...], b_ref[...]).astype(BF16)

        load_w.wait()
        order = plane_order(me)
        sends = []
        for n, (i, j, row, column) in enumerate(order):
            if j == 0:
                for part_index in range(3):
                    at = pl.multiple_of(part_index * width + row * 256, 256)
                    out = (
                        jnp.dot(normed, wq[:, pl.ds(at, 256)], preferred_element_type=F32)
                        + qb_ref[:, pl.ds(at, 256)]
                    )
                    if part_index == 0:
                        out = out * scale
                    turned = out.T.astype(BF16)
                    for k in range(ROW):
                        blocks[
                            row * ROW + k, part_index * HEAD : (part_index + 1) * HEAD, :
                        ] = turned[k * HEAD : (k + 1) * HEAD, :]
            head = row * ROW + column
            q_src = blocks.at[head, 0:HEAD]
            kv_src = blocks.at[head, HEAD : 3 * HEAD]
            if n == 0:
                own_q = pltpu.make_async_copy(q_src, q_ref.at[here], load.at[2])
                own_kv = pltpu.make_async_copy(kv_src, kv_ref.at[0, here], load.at[3])
                own_q.start()
                own_kv.start()
            else:
                to = half * PLANE + head
                kv_copy = remote(kv_src, kv_ref.at[0, here], kv_s.at[n], kv_r.at[n], to)
                q_copy = remote(q_src, q_ref.at[here], q_s.at[n], q_r.at[n], to)
                kv_copy.start()
                q_copy.start()
                sends.append((kv_copy, q_copy))

        y, x = lax.rem(lax.div(me, ROW), ROW), lax.rem(me, ROW)
        beside = (1 - half) * PLANE + here
        forwards = []
        for n, (i, j, _, _) in enumerate(order):
            source = lax.rem(y + ROW - i, ROW) * ROW + lax.rem(x + ROW - j, ROW)
            if n == 0:
                passed = remote(
                    blocks.at[here, HEAD : 3 * HEAD], kv_ref.at[1, here], f_s.at[n], f_r.at[n], beside
                )
            else:
                remote(
                    blocks.at[here, HEAD : 3 * HEAD],
                    kv_ref.at[0, source],
                    kv_s.at[n],
                    kv_r.at[n],
                    me,
                ).wait_recv()
                passed = remote(
                    kv_ref.at[0, source], kv_ref.at[1, source], f_s.at[n], f_r.at[n], beside
                )
            passed.start()
            forwards.append(passed)
        own_q.wait()
        own_kv.wait()
        for kv_copy, q_copy in sends:
            q_copy.wait()
            kv_copy.wait_send()
        for passed in forwards:
            passed.wait()

    vmem = pl.BlockSpec(memory_space=pltpu.VMEM)
    anywhere = pl.BlockSpec(memory_space=pl.ANY)
    dma = pltpu.SemaphoreType.DMA
    return pl.pallas_call(
        kernel,
        in_specs=[vmem, vmem, vmem, anywhere, vmem, vmem, anywhere, vmem],
        out_specs=[vmem, anywhere, anywhere],
        out_shape=[
            jax.ShapeDtypeStruct((tokens, width), BF16),
            jax.ShapeDtypeStruct((PLANE, HEAD, tokens), BF16),
            jax.ShapeDtypeStruct((2, PLANE, 2 * HEAD, tokens), BF16),
        ],
        scratch_shapes=[
            pltpu.VMEM((8, 128), F32),
            pltpu.VMEM((count - 1, 8, 128), F32),
            pltpu.VMEM((2, side, side), F32),
            pltpu.VMEM((6 * pad, 128), F32),
            pltpu.VMEM((tokens, 6 * 128), BF16),
            pltpu.VMEM((6 * 128, width), BF16),
            pltpu.VMEM(w_qkv.shape, BF16),
            pltpu.VMEM(pos.shape, BF16),
            pltpu.VMEM((HEADS, 3 * HEAD, tokens), BF16),
            dma((count - 1,)), dma((count - 1,)), dma((2,)), dma((2,)),
            dma((PLANE,)), dma((PLANE,)), dma((PLANE,)), dma((PLANE,)),
            dma((PLANE,)), dma((PLANE,)), dma((4,)),
        ],
        compiler_params=pltpu.CompilerParams(
            vmem_limit_bytes=VMEM_LIMIT, collective_id=0, has_side_effects=True
        ),
        name="front",
    )(density, stem_weight, stem_bias, pos, gain, shift, w_qkv, qkv_bias)


def attention(query, keys_values):
    parts, _, tokens = query.shape
    sources = keys_values.shape[0]
    keys = sources * tokens
    group = 4
    width = group * tokens
    chunk = 512
    steps = keys // chunk

    def kernel(q_ref, kv_ref, o_ref, k_s, v_s, s_s):
        @pl.when(pl.program_id(0) == 0)
        def _():
            for i in range(sources):
                at = i * tokens
                k_s[at : at + tokens, :] = kv_ref[i, 0:HEAD, :].T
                v_s[0:HEAD, at : at + tokens] = kv_ref[i, HEAD : 2 * HEAD, :]
            row = lax.broadcasted_iota(jnp.int32, (VROWS - HEAD, keys), 0)
            v_s[HEAD:VROWS, :] = jnp.where(row == 0, 1.0, 0.0).astype(BF16)

        q = jnp.concatenate([q_ref[i] for i in range(group)], axis=1)

        def scores(c):
            at = pl.multiple_of(c * chunk, chunk)
            return jnp.dot(k_s[pl.ds(at, chunk), :], q, preferred_element_type=F32)

        first = scores(0)
        s_s[0] = first
        top = jnp.max(first, axis=0, keepdims=True)

        def body(i, carry):
            high, total, top = carry
            for slot in range(2):
                c = 2 * i + slot
                raised = jnp.maximum(high, top)
                fade = jnp.exp2(high - raised)
                weights = jnp.exp2(s_s[slot] - raised).astype(BF16)
                at = pl.multiple_of(c * chunk, chunk)
                ahead = scores(jnp.minimum(c + 1, steps - 1))
                s_s[1 - slot] = ahead
                top = jnp.max(ahead, axis=0, keepdims=True)
                total = total * fade + jnp.dot(
                    v_s[:, pl.ds(at, chunk)], weights, preferred_element_type=F32
                )
                high = raised
            return high, total, top

        _, total, _ = lax.fori_loop(
            0,
            steps // 2,
            body,
            (jnp.full((1, width), -1e30, F32), jnp.zeros((VROWS, width), F32), top),
        )
        mixed = (total[0:HEAD] / total[HEAD : HEAD + 1]).astype(BF16)
        for i in range(group):
            o_ref[i] = mixed[:, i * tokens : (i + 1) * tokens]

    whole = pl.BlockSpec(keys_values.shape, lambda i: (0, 0, 0))
    block = pl.BlockSpec((group, HEAD, tokens), lambda i: (i, 0, 0))
    return pl.pallas_call(
        kernel,
        grid=(parts // group,),
        in_specs=[block, whole],
        out_specs=block,
        out_shape=jax.ShapeDtypeStruct(query.shape, BF16),
        scratch_shapes=[
            pltpu.VMEM((keys, HEAD), BF16),
            pltpu.VMEM((VROWS, keys), BF16),
            pltpu.VMEM((2, chunk, width), F32),
        ],
        compiler_params=pltpu.CompilerParams(vmem_limit_bytes=VMEM_LIMIT),
        name="attention",
    )(query, keys_values)


def tail(mixed, residual, w_out, out_bias, gain, shift, w1, b1, w2, b2):
    tokens, width = residual.shape
    hidden_width = w1.shape[1]
    step = 512

    def kernel(
        o_ref, res_ref, wo_ref, ob_ref, g_ref, b_ref, w1_ref, b1_ref, w2_ref, b2_ref,
        out_ref,
        att, wo, w1v, w2v, send, recv, load,
    ):
        me = lax.axis_index("ctx")
        half = lax.div(me, PLANE)
        here = lax.rem(me, PLANE)
        order = plane_order(me)
        targets = [half * PLANE + row * ROW + column for _, _, row, column in order]
        barrier = greet(targets[1:])
        loads = [
            pltpu.make_async_copy(wo_ref, wo, load.at[0]),
            pltpu.make_async_copy(w1_ref, w1v, load.at[1]),
            pltpu.make_async_copy(w2_ref, w2v, load.at[2]),
        ]
        for copy in loads:
            copy.start()
        own = pltpu.make_async_copy(o_ref.at[here], att.at[here], load.at[3])
        own.start()
        pl.semaphore_wait(barrier, PLANE - 1)
        sends = []
        for n, (_, _, row, column) in enumerate(order):
            if n:
                copy = remote(
                    o_ref.at[row * ROW + column], att.at[here], send.at[n], recv.at[n], targets[n]
                )
                copy.start()
                sends.append(copy)
        own.wait()
        for copy in sends:
            copy.wait()
        loads[0].wait()
        attended = att[...].reshape(width, tokens).T
        stream = (
            res_ref[...].astype(F32)
            + jnp.dot(attended, wo[...], preferred_element_type=F32)
            + ob_ref[...]
        ).astype(BF16)
        rows = stream.astype(F32)
        normed = normalize(rows, g_ref[...], b_ref[...]).astype(BF16)
        loads[1].wait()
        loads[2].wait()

        def body(c, total):
            at = pl.multiple_of(c * step, step)
            hidden = (
                jnp.dot(normed, w1v[:, pl.ds(at, step)], preferred_element_type=F32)
                + b1_ref[:, pl.ds(at, step)]
            )
            hidden = 0.5 * hidden * (1.0 + lax.erf(hidden * math.sqrt(0.5)))
            return total + jnp.dot(
                hidden.astype(BF16), w2v[pl.ds(at, step), :], preferred_element_type=F32
            )

        total = lax.fori_loop(0, hidden_width // step, body, rows + b2_ref[...])
        out_ref[...] = total.astype(BF16)

    vmem = pl.BlockSpec(memory_space=pltpu.VMEM)
    anywhere = pl.BlockSpec(memory_space=pl.ANY)
    dma = pltpu.SemaphoreType.DMA
    return pl.pallas_call(
        kernel,
        in_specs=[vmem, vmem, anywhere, vmem, vmem, vmem, anywhere, vmem, anywhere, vmem],
        out_specs=vmem,
        out_shape=jax.ShapeDtypeStruct((tokens, width), BF16),
        scratch_shapes=[
            pltpu.VMEM(mixed.shape, BF16),
            pltpu.VMEM(w_out.shape, BF16),
            pltpu.VMEM(w1.shape, BF16),
            pltpu.VMEM(w2.shape, BF16),
            dma((PLANE,)), dma((PLANE,)), dma((4,)),
        ],
        compiler_params=pltpu.CompilerParams(
            vmem_limit_bytes=VMEM_LIMIT, collective_id=1, has_side_effects=True
        ),
        name="tail",
    )(mixed, residual, w_out, out_bias, gain, shift, w1, b1, w2, b2)


def per_device(
    density, stem_weight, stem_bias, pos_embed, ln1_gain, ln1_bias, w_qkv, qkv_bias,
    w_out, out_bias, ln2_gain, ln2_bias, w_fc1, fc1_bias, w_fc2, fc2_bias,
):
    def flat(vector):
        return vector.reshape(1, -1)

    cells = float(density.size * lax.axis_size("ctx"))
    residual, query, keys_values = front(
        density, stem_weight, flat(stem_bias), pos_embed, flat(ln1_gain), flat(ln1_bias),
        w_qkv, flat(qkv_bias), cells,
    )
    mixed = attention(query, keys_values.reshape(2 * PLANE, 2 * HEAD, -1))
    return tail(
        mixed, residual, w_out, flat(out_bias), flat(ln2_gain), flat(ln2_bias),
        w_fc1, flat(fc1_bias), w_fc2, flat(fc2_bias),
    )


def solution(mesh):
    in_specs = (P(("dp", "ctx"), None, None), P(), P(), P("ctx", None)) + (P(),) * 12
    return jax.shard_map(
        per_device, mesh=mesh, in_specs=in_specs, out_specs=P(("dp", "ctx"), None), check_vma=False
    )
```

profile of v0, /device:TPU:0, one launch (start us, length us, event | category | flops | bytes accessed | tf_op | source)
XLA Modules:
  0.0 109.2 jit_solution(6061105693302699207)
XLA Ops:
  0.0 45.1 %front.1 = (bf16[256,1024]{1,0:T(8,128)(2,1)}, bf16[16,64,256]{2,1,0:T(8,128)(2,1)}, bf16[2,16,128,256]{3,2,1,0:T(8,128)(2,1)}) custom-call(f32[4,64,64]{2,1,0:T(8,128)} %d_ref.1, bf16[216,1024]{1,0:T(8,128)(2,1)} %ws_ref.1, f32[1,1024]{1,0:T(1,128)} %bitcast.13, bf16[256,1024]{1,0:T(8,128)(2,1)} %pos_ref.1, f32[1,1024]{1,0:T(1,128)} %bitcast.14, ...), custom_call_target="tpu_custom_call" | custom-call | tf_op jit(solution)/shard_map/front/pallas_call | solution.py:228
  45.2 40.4 %attention.1.o_ref = bf16[16,64,256]{2,1,0:T(8,128)(2,1)} custom-call(bf16[16,64,256]{2,1,0:T(8,128)(2,1)} %get-tuple-element.8.q_ref, bf16[32,128,256]{2,1,0:T(8,128)(2,1)} %bitcast.10), custom_call_target="tpu_custom_call" | custom-call | tf_op jit(solution)/shard_map/attention/pallas_call | solution.py:316
  85.6 21.7 %tail.1 = bf16[256,1024]{1,0:T(8,128)(2,1)} custom-call(bf16[16,64,256]{2,1,0:T(8,128)(2,1)} %attention.1.o_ref, bf16[256,1024]{1,0:T(8,128)(2,1)} %get-tuple-element.10.res_ref, bf16[1024,1024]{1,0:T(8,128)(2,1)} %wo_ref.1, f32[1,1024]{1,0:T(1,128)} %bitcast.16, f32[1,1024]{1,0:T(1,128)} %bitcast.17, f32[1,1024]{1,0:T(1,128)} %bitcast.18, ...), custom_call_target="tpu_custom_call" | custom-call | tf_op jit(solution)/shard_map/tail/pallas_call | solution.py:398
  107.3 1.9 %copy.18 = bf16[256,1024]{1,0:T(8,128)(2,1)} copy(bf16[256,1024]{1,0:T(8,128)(2,1)} %tail.1) | data formatting | bytes 1048576
where the time goes:
time: 109 us
  Pallas kernels  107 us (98%)
  local copies, waits for them, and re-layouts  1.87 us (2%)
    pallas_call x1, Pallas kernels, front(): pl.pallas_call(kernel, in_specs=[vmem, vmem, vmem, anywhere, vmem, vmem,...  45.1 us
    pallas_call x1, Pallas kernels, attention(): pl.pallas_call(kernel, grid=(parts // group,), in_specs=[block, whole], o...  40.4 us
    pallas_call x1, Pallas kernels, tail(): pl.pallas_call(kernel, in_specs=[vmem, vmem, anywhere, vmem, vmem, vmem,...  21.7 us

commit v1 on v0

v1 whole, which is shorter than its diff:
```python
import math

import jax
import jax.numpy as jnp
from jax import lax
from jax.experimental import pallas as pl
from jax.experimental.pallas import tpu as pltpu
from jax.sharding import PartitionSpec as P

F32 = jnp.float32
BF16 = jnp.bfloat16
HEADS = 16
HEAD = 64
VROWS = 80
PLANE = 16
ROW = 4
MESH = pl.DeviceIdType.MESH
VMEM_LIMIT = 58 * 2**20


def remote(src, dst, send, recv, index):
    return pltpu.make_async_remote_copy(
        src_ref=src,
        dst_ref=dst,
        send_sem=send,
        recv_sem=recv,
        device_id={"ctx": index},
        device_id_type=MESH,
    )


def greet(peers):
    barrier = pltpu.get_barrier_semaphore()
    for peer in peers:
        pl.semaphore_signal(barrier, inc=1, device_id={"ctx": peer}, device_id_type=MESH)
    return barrier


def normalize(rows, gain, shift):
    center = rows - jnp.mean(rows, axis=-1, keepdims=True)
    spread = jnp.mean(center * center, axis=-1, keepdims=True)
    return center * lax.rsqrt(spread + 1e-06) * gain + shift


def plane_order(me):
    y, x = lax.rem(lax.div(me, ROW), ROW), lax.rem(me, ROW)
    order = []
    for i in (0, 1, 3, 2):
        for j in range(ROW):
            order.append((i, j, lax.rem(y + i, ROW), lax.rem(x + j, ROW)))
    return order


def encoder(
    density, stem_weight, stem_bias, pos, gain1, shift1, w_qkv, qkv_bias,
    w_out, out_bias, gain2, shift2, w1, b1, w2, b2, cells,
):
    planes, side, _ = density.shape
    count = lax.axis_size("ctx")
    width = stem_weight.shape[1]
    hidden_width = w1.shape[1]
    tokens = pos.shape[0]
    grid = side // 4
    lanes = grid * 128
    scale = math.log2(math.e) / math.sqrt(HEAD)
    pad = 72
    stages = 2 * ROW
    queries = ROW * tokens
    chunk = 2 * tokens
    step = 512

    def kernel(
        d_ref, ws_ref, sb_ref, pos_ref, g1_ref, s1_ref, wq_ref, qb_ref,
        wo_ref, ob_ref, g2_ref, s2_ref, w1_ref, b1_ref, w2_ref, b2_ref,
        out_ref,
        mine, sums, halo, fp, x6, w6, wq, posv, wo, w1v, w2v, resv,
        q_out, kv_out, q_in, kv_in, score, high_s, total_s, o_out, att,
        sum_s, sum_r, halo_s, halo_r, q_s, q_r, kv_s, kv_r, f_s, f_r, o_s, o_r, load,
    ):
        me = lax.axis_index("ctx")
        half = lax.div(me, PLANE)
        here = lax.rem(me, PLANE)
        y, x = lax.div(here, ROW), lax.rem(here, ROW)
        beside = (1 - half) * PLANE + here
        peers = [lax.rem(me + i, count) for i in range(1, count)]
        barrier = greet(peers)
        load_w = pltpu.make_async_copy(wq_ref, wq, load.at[0])
        load_w.start()
        load_p = pltpu.make_async_copy(pos_ref, posv, load.at[1])
        load_p.start()

        slab = d_ref[...]
        part = jnp.sum(slab, axis=0)
        part = jnp.sum(part, axis=0, keepdims=True)
        part = jnp.sum(part, axis=1, keepdims=True)
        mine[...] = jnp.broadcast_to(part, (8, 128))
        fp[...] = jnp.zeros(fp.shape, F32)
        w6[...] = jnp.zeros(w6.shape, BF16)
        for a in range(6):
            w6[a * 128 : a * 128 + 36, :] = ws_ref[a * 36 : (a + 1) * 36, :]
        pl.semaphore_wait(barrier, count - 1)

        up, down = peers[0], peers[-1]
        to_up = remote(d_ref.at[planes - 1], halo.at[0], halo_s.at[0], halo_r.at[0], up)
        to_down = remote(d_ref.at[0], halo.at[1], halo_s.at[1], halo_r.at[1], down)
        to_up.start()
        to_down.start()
        shares = []
        for i, peer in enumerate(peers):
            shares.append(remote(mine, sums.at[i], sum_s.at[i], sum_r.at[i], peer))
            shares[-1].start()
        for i in range(PLANE):
            q_in[i, 0:HEAD, :] = jnp.zeros((HEAD, tokens), BF16)
            q_in[i, 2 * HEAD : 3 * HEAD, :] = jnp.zeros((HEAD, tokens), BF16)
        for share in shares:
            share.wait()
        to_up.wait()
        to_down.wait()
        total = mine[...] + jnp.sum(sums[...], axis=0)
        mean = (total / cells)[0:1, 0:1]

        def logged(values):
            return jnp.log(values / mean).astype(BF16).astype(F32)

        low = jnp.where(me > 0, logged(halo[0]), 0.0)
        high = jnp.where(me < count - 1, logged(halo[1]), 0.0)
        own = logged(slab.reshape(planes * side, side))
        fp[1 : 1 + side, 0:side] = low
        for a in range(planes):
            at = (a + 1) * pad + 1
            fp[at : at + side, 0:side] = own[a * side : (a + 1) * side, :]
        at = (planes + 1) * pad + 1
        fp[at : at + side, 0:side] = high

        z = lax.broadcasted_iota(jnp.int32, (side, lanes), 0)
        col = lax.broadcasted_iota(jnp.int32, (side, lanes), 1)
        lane = jnp.bitwise_and(col, 127)
        base = z + 1 - 4 * jnp.right_shift(col, 7) - lane
        spread = jnp.zeros((6 * grid, lanes), F32)
        for b in range(6):
            rows = jnp.concatenate(
                [fp[pl.ds(a * pad + b, grid, stride=4), 0:side] for a in range(6)], axis=0
            )
            pick = (base == -6 * b) & (lane >= 6 * b) & (lane < 6 * b + 6)
            spread += jnp.dot(
                rows.astype(BF16),
                jnp.where(pick, 1.0, 0.0).astype(BF16),
                preferred_element_type=F32,
            )
        spread = spread.astype(BF16)
        for k in range(grid):
            for a in range(6):
                x6[k * grid : (k + 1) * grid, a * 128 : (a + 1) * 128] = spread[
                    a * grid : (a + 1) * grid, k * 128 : (k + 1) * 128
                ]
        r = lax.broadcasted_iota(jnp.int32, (tokens, tokens), 0)
        s = lax.broadcasted_iota(jnp.int32, (tokens, tokens), 1)
        turn = (jnp.right_shift(r, 4) == jnp.bitwise_and(s, 15)) & (
            jnp.bitwise_and(r, 15) == jnp.right_shift(s, 4)
        )
        patches = jnp.dot(
            jnp.where(turn, 1.0, 0.0).astype(BF16), x6[...], preferred_element_type=F32
        ).astype(BF16)
        load_p.wait()
        embedded = (
            jnp.dot(patches, w6[...], preferred_element_type=F32)
            + sb_ref[...]
            + posv[...].astype(F32)
        )
        residual = embedded.astype(BF16)
        resv[...] = residual
        normed = normalize(residual.astype(F32), g1_ref[...], s1_ref[...]).astype(BF16)

        load_w.wait()
        loads = [
            pltpu.make_async_copy(wo_ref, wo, load.at[2]),
            pltpu.make_async_copy(w1_ref, w1v, load.at[3]),
            pltpu.make_async_copy(w2_ref, w2v, load.at[4]),
        ]
        left = lax.broadcasted_iota(jnp.int32, (128, 128), 1) < HEAD
        order = plane_order(me)

        def project(part_index, row):
            at = pl.multiple_of(part_index * width + row * 256, 256)
            return (
                jnp.dot(normed, wq[:, pl.ds(at, 256)], preferred_element_type=F32)
                + qb_ref[:, pl.ds(at, 256)]
            )

        def make_q(row):
            turned = (project(0, row) * scale).T.astype(BF16)
            for k in range(ROW):
                q_out[row * ROW + k] = turned[k * HEAD : (k + 1) * HEAD, :]

        def make_kv(row):
            keys = project(1, row)
            turned = project(2, row).T.astype(BF16)
            for k in range(ROW):
                pair = keys[:, (k // 2) * 128 : (k // 2 + 1) * 128]
                lo, hi = pair[0:128], pair[128:256]
                if k % 2 == 0:
                    packed = jnp.where(left, lo, pltpu.roll(hi, HEAD, 1))
                else:
                    packed = jnp.where(left, pltpu.roll(lo, HEAD, 1), hi)
                at = row * ROW + k
                kv_out[at, 0:128, :] = packed.astype(BF16)
                kv_out[at, 128 : 128 + HEAD, :] = turned[k * HEAD : (k + 1) * HEAD, 0:128]
                kv_out[at, 128 + HEAD : 256, :] = turned[k * HEAD : (k + 1) * HEAD, 128:256]

        def q_copy(n):
            head = order[n][2] * ROW + order[n][3]
            return remote(
                q_out.at[head], q_in.at[n, HEAD : 2 * HEAD], q_s.at[n], q_r.at[n], half * PLANE + head
            )

        def kv_copy(n):
            head = order[n][2] * ROW + order[n][3]
            return remote(kv_out.at[head], kv_in.at[n], kv_s.at[n], kv_r.at[n], half * PLANE + head)

        for g in range(ROW):
            row = order[g * ROW][2]
            make_q(row)
            for n in range(g * ROW, (g + 1) * ROW):
                if n:
                    q_copy(n).start()
            if g == 0:
                make_kv(row)
                for n in range(1, ROW):
                    kv_copy(n).start()
        q_in[0, HEAD : 2 * HEAD, :] = q_out[here]
        kv_in[0] = kv_out[here]
        for g in range(1, ROW):
            make_kv(order[g * ROW][2])
            for n in range(g * ROW, (g + 1) * ROW):
                kv_copy(n).start()
        for copy in loads:
            copy.start()

        def forward(n):
            return remote(kv_in.at[n], kv_in.at[PLANE + n], f_s.at[n], f_r.at[n], beside)

        def arrived(n):
            remote(kv_in.at[n], kv_in.at[n], kv_s.at[n], kv_r.at[n], beside).wait_recv()

        def asked(n):
            remote(
                q_in.at[n, HEAD : 2 * HEAD], q_in.at[n, HEAD : 2 * HEAD], q_s.at[n], q_r.at[n], beside
            ).wait_recv()

        remote(kv_out.at[here], kv_in.at[PLANE], f_s.at[0], f_r.at[0], beside).start()
        for n in range(1, ROW):
            asked(n)
            arrived(n)
            forward(n).start()

        ones = jnp.where(
            lax.broadcasted_iota(jnp.int32, (VROWS - HEAD, 128), 0) == 0, 1.0, 0.0
        ).astype(BF16)

        def scores(u, c):
            g = lax.rem(u, ROW)
            n = lax.div(u, ROW) * ROW + 2 * c
            keys = kv_in[pl.ds(n, 2), 0:128, :].reshape(256, 128)
            lo = jnp.concatenate([q_in[g * ROW + k, HEAD : 3 * HEAD, :] for k in range(ROW)], axis=1)
            hi = jnp.concatenate([q_in[g * ROW + k, 0 : 2 * HEAD, :] for k in range(ROW)], axis=1)
            return jnp.concatenate(
                [
                    jnp.dot(keys, lo, preferred_element_type=F32),
                    jnp.dot(keys, hi, preferred_element_type=F32),
                ],
                axis=0,
            )

        def values(u, c):
            n = lax.div(u, ROW) * ROW + 2 * c
            pieces = []
            for at in (128, 128 + HEAD):
                for k in range(2):
                    pieces.append(
                        jnp.concatenate([kv_in[n + k, at : at + HEAD, :], ones], axis=0)
                    )
            return jnp.concatenate(pieces, axis=1)

        for g in range(ROW):
            high_s[g] = jnp.full((1, queries), -1e30, F32)
            total_s[g] = jnp.zeros((VROWS, queries), F32)
        first = scores(0, 0)
        score[0] = first

        def body(u, top):
            stage = lax.div(u, ROW)
            g = lax.rem(u, ROW)

            @pl.when((stage == 0) & (g < ROW - 1))
            def _():
                for k in range(ROW):
                    asked((g + 1) * ROW + k)

            @pl.when((g == ROW - 1) & (stage < ROW - 1))
            def _():
                for k in range(ROW):
                    n = (stage + 1) * ROW + k
                    arrived(n)
                    forward(n).start()

            @pl.when((g == ROW - 1) & (stage >= ROW - 1) & (stage < stages - 1))
            def _():
                for k in range(ROW):
                    forward((stage + 1 - ROW) * ROW + k).wait_recv()

            highest = high_s[g]
            total = total_s[g]
            for slot in range(2):
                raised = jnp.maximum(highest, top)
                fade = jnp.exp2(highest - raised)
                weights = jnp.exp2(score[slot] - raised).astype(BF16)
                if slot == 0:
                    ahead = scores(u, 1)
                else:
                    ahead = scores(jnp.minimum(u + 1, stages * ROW - 1), 0)
                score[1 - slot] = ahead
                top = jnp.max(ahead, axis=0, keepdims=True)
                total = total * fade + jnp.dot(
                    values(u, slot), weights, preferred_element_type=F32
                )
                highest = raised
            high_s[g] = highest
            total_s[g] = total

            @pl.when(stage == stages - 1)
            def _():
                final = total_s[g]
                mixed = (final[0:HEAD] / final[HEAD : HEAD + 1]).astype(BF16)
                row_step = g + jnp.where(g == 2, 1, 0) - jnp.where(g == 3, 1, 0)
                source_row = lax.rem(y + ROW - row_step, ROW)
                for k in range(ROW):
                    n = g * ROW + k
                    o_out[n] = mixed[:, k * tokens : (k + 1) * tokens]
                    source = source_row * ROW + lax.rem(x + ROW - k, ROW)
                    back = remote(
                        o_out.at[n], att.at[here], o_s.at[n], o_r.at[n], half * PLANE + source
                    )
                    if k == 0:

                        @pl.when(g > 0)
                        def _():
                            back.start()
                    else:
                        back.start()

            return top

        lax.fori_loop(0, stages * ROW, body, jnp.max(first, axis=0, keepdims=True))
        att[here] = o_out[0]

        def returned(n):
            head = order[n][2] * ROW + order[n][3]
            return remote(o_out.at[n], att.at[head], o_s.at[n], o_r.at[n], beside)

        for n in range(1, PLANE):
            returned(n).wait_recv()
        loads[0].wait()
        attended = att[...].reshape(width, tokens).T
        stream = (
            resv[...].astype(F32)
            + jnp.dot(attended, wo[...], preferred_element_type=F32)
            + ob_ref[...]
        ).astype(BF16)
        rows = stream.astype(F32)
        normed_two = normalize(rows, g2_ref[...], s2_ref[...]).astype(BF16)
        loads[1].wait()
        loads[2].wait()

        def mlp(c, total):
            at = pl.multiple_of(c * step, step)
            hidden = (
                jnp.dot(normed_two, w1v[:, pl.ds(at, step)], preferred_element_type=F32)
                + b1_ref[:, pl.ds(at, step)]
            )
            hidden = 0.5 * hidden * (1.0 + lax.erf(hidden * math.sqrt(0.5)))
            return total + jnp.dot(
                hidden.astype(BF16), w2v[pl.ds(at, step), :], preferred_element_type=F32
            )

        out_ref[...] = lax.fori_loop(0, hidden_width // step, mlp, rows + b2_ref[...]).astype(BF16)
        for n in range(1, PLANE):
            q_copy(n).wait_send()
            kv_copy(n).wait_send()
            returned(n).wait_send()
        for n in range(PLANE):
            forward(n).wait_send()

    vmem = pl.BlockSpec(memory_space=pltpu.VMEM)
    anywhere = pl.BlockSpec(memory_space=pl.ANY)
    dma = pltpu.SemaphoreType.DMA
    return pl.pallas_call(
        kernel,
        in_specs=[
            vmem, vmem, vmem, anywhere, vmem, vmem, anywhere, vmem,
            anywhere, vmem, vmem, vmem, anywhere, vmem, anywhere, vmem,
        ],
        out_specs=vmem,
        out_shape=jax.ShapeDtypeStruct((tokens, width), BF16),
        scratch_shapes=[
            pltpu.VMEM((8, 128), F32),
            pltpu.VMEM((count - 1, 8, 128), F32),
            pltpu.VMEM((2, side, side), F32),
            pltpu.VMEM((6 * pad, 128), F32),
            pltpu.VMEM((tokens, 6 * 128), BF16),
            pltpu.VMEM((6 * 128, width), BF16),
            pltpu.VMEM(w_qkv.shape, BF16),
            pltpu.VMEM(pos.shape, BF16),
            pltpu.VMEM(w_out.shape, BF16),
            pltpu.VMEM(w1.shape, BF16),
            pltpu.VMEM(w2.shape, BF16),
            pltpu.VMEM((tokens, width), BF16),
            pltpu.VMEM((HEADS, HEAD, tokens), BF16),
            pltpu.VMEM((HEADS, 256, 128), BF16),
            pltpu.VMEM((PLANE, 3 * HEAD, tokens), BF16),
            pltpu.VMEM((2 * PLANE, 256, 128), BF16),
            pltpu.VMEM((2, chunk, queries), F32),
            pltpu.VMEM((ROW, 1, queries), F32),
            pltpu.VMEM((ROW, VROWS, queries), F32),
            pltpu.VMEM((PLANE, HEAD, tokens), BF16),
            pltpu.VMEM((HEADS, HEAD, tokens), BF16),
            dma((count - 1,)), dma((count - 1,)), dma((2,)), dma((2,)),
            dma((PLANE,)), dma((PLANE,)), dma((PLANE,)), dma((PLANE,)),
            dma((PLANE,)), dma((PLANE,)), dma((PLANE,)), dma((PLANE,)), dma((5,)),
        ],
        compiler_params=pltpu.CompilerParams(
            vmem_limit_bytes=VMEM_LIMIT, collective_id=0, has_side_effects=True
        ),
        name="encoder",
    )(
        density, stem_weight, stem_bias, pos, gain1, shift1, w_qkv, qkv_bias,
        w_out, out_bias, gain2, shift2, w1, b1, w2, b2,
    )


def per_device(
    density, stem_weight, stem_bias, pos_embed, ln1_gain, ln1_bias, w_qkv, qkv_bias,
    w_out, out_bias, ln2_gain, ln2_bias, w_fc1, fc1_bias, w_fc2, fc2_bias,
):
    def flat(vector):
        return vector.reshape(1, -1)

    return encoder(
        density, stem_weight, flat(stem_bias), pos_embed, flat(ln1_gain), flat(ln1_bias),
        w_qkv, flat(qkv_bias), w_out, flat(out_bias), flat(ln2_gain), flat(ln2_bias),
        w_fc1, flat(fc1_bias), w_fc2, flat(fc2_bias),
        float(density.size * lax.axis_size("ctx")),
    )


def solution(mesh):
    in_specs = (P(("dp", "ctx"), None, None), P(), P(), P("ctx", None)) + (P(),) * 12
    return jax.shard_map(
        per_device, mesh=mesh, in_specs=in_specs, out_specs=P(("dp", "ctx"), None), check_vma=False
    )
```

time: 109 us -> 91.2 us (0.84); the launches traced: 109 us -> 89.7 us
  Pallas kernels: 107 us -> 87.8 us
    pallas_call x3 -> x1, Pallas kernels: 107 us -> 87.8 us  [encoder(): pl.pallas_call(kernel, in_specs=[vmem, vmem, vmem, anywhere, vmem, vmem,...]
where the time goes in v1:
time: 91.2 us; the launch traced here: 89.7 us
  Pallas kernels  87.8 us (96%)
  local copies, waits for them, and re-layouts  1.87 us (2%)
    pallas_call x1, Pallas kernels, encoder(): pl.pallas_call(kernel, in_specs=[vmem, vmem, vmem, anywhere, vmem, vmem,...  87.8 us
    unnamed x1, local copies, waits for them, and re-layouts  1.87 us

profile of v1, /device:TPU:0, one launch (start us, length us, event | category | flops | bytes accessed | tf_op | source)
XLA Modules:
  0.0 89.7 jit_solution(4708092998114220545)
XLA Ops:
  0.0 87.8 %encoder.1 = bf16[256,1024]{1,0:T(8,128)(2,1)} custom-call(f32[4,64,64]{2,1,0:T(8,128)} %d_ref.1, bf16[216,1024]{1,0:T(8,128)(2,1)} %ws_ref.1, f32[1,1024]{1,0:T(1,128)} %bitcast.11, bf16[256,1024]{1,0:T(8,128)(2,1)} %pos_ref.1, f32[1,1024]{1,0:T(1,128)} %bitcast.12, f32[1,1024]{1,0:T(1,128)} %bitcast.13, bf16[1024,3072]{1,0:T(8,128)(2,1)} %wq_ref.1, ...), custom_call_target="tpu_custom_call" | custom-call | tf_op jit(solution)/shard_map/encoder/pallas_call | solution.py:396
  87.8 1.9 %copy.18 = bf16[256,1024]{1,0:T(8,128)(2,1)} copy(bf16[256,1024]{1,0:T(8,128)(2,1)} %encoder.1) | data formatting | bytes 1048576

commit v2 on v1

--- a/solution.py
+++ b/solution.py
@@ -65,8 +65,10 @@
     scale = math.log2(math.e) / math.sqrt(HEAD)
     pad = 72
     stages = 2 * ROW
-    queries = ROW * tokens
+    group = 2 * ROW
+    queries = group * tokens
     chunk = 2 * tokens
+    strip = 512
     step = 512
 
     def kernel(
@@ -217,24 +219,19 @@
             head = order[n][2] * ROW + order[n][3]
             return remote(kv_out.at[head], kv_in.at[n], kv_s.at[n], kv_r.at[n], half * PLANE + head)
 
+        make_kv(order[0][2])
+        kv_in[0] = kv_out[here]
+        for n in range(1, ROW):
+            kv_copy(n).start()
+        remote(kv_out.at[here], kv_in.at[PLANE], f_s.at[0], f_r.at[0], beside).start()
         for g in range(ROW):
-            row = order[g * ROW][2]
-            make_q(row)
+            make_q(order[g * ROW][2])
             for n in range(g * ROW, (g + 1) * ROW):
                 if n:
                     q_copy(n).start()
-            if g == 0:
-                make_kv(row)
-                for n in range(1, ROW):
-                    kv_copy(n).start()
         q_in[0, HEAD : 2 * HEAD, :] = q_out[here]
-        kv_in[0] = kv_out[here]
         for g in range(1, ROW):
             make_kv(order[g * ROW][2])
-            for n in range(g * ROW, (g + 1) * ROW):
-                kv_copy(n).start()
-        for copy in loads:
-            copy.start()
 
         def forward(n):
             return remote(kv_in.at[n], kv_in.at[PLANE + n], f_s.at[n], f_r.at[n], beside)
@@ -247,32 +244,41 @@
                 q_in.at[n, HEAD : 2 * HEAD], q_in.at[n, HEAD : 2 * HEAD], q_s.at[n], q_r.at[n], beside
             ).wait_recv()
 
-        remote(kv_out.at[here], kv_in.at[PLANE], f_s.at[0], f_r.at[0], beside).start()
         for n in range(1, ROW):
-            asked(n)
             arrived(n)
             forward(n).start()
+        for n in range(1, ROW):
+            kv_copy(n).wait_send()
+        for n in range(1, PLANE):
+            q_copy(n).wait_send()
+        for n in range(ROW, 3 * ROW):
+            kv_copy(n).start()
+        for copy in loads:
+            copy.start()
+        for n in range(1, PLANE):
+            asked(n)
 
         ones = jnp.where(
             lax.broadcasted_iota(jnp.int32, (VROWS - HEAD, 128), 0) == 0, 1.0, 0.0
         ).astype(BF16)
 
-        def scores(u, c):
-            g = lax.rem(u, ROW)
-            n = lax.div(u, ROW) * ROW + 2 * c
-            keys = kv_in[pl.ds(n, 2), 0:128, :].reshape(256, 128)
-            lo = jnp.concatenate([q_in[g * ROW + k, HEAD : 3 * HEAD, :] for k in range(ROW)], axis=1)
-            hi = jnp.concatenate([q_in[g * ROW + k, 0 : 2 * HEAD, :] for k in range(ROW)], axis=1)
-            return jnp.concatenate(
-                [
-                    jnp.dot(keys, lo, preferred_element_type=F32),
-                    jnp.dot(keys, hi, preferred_element_type=F32),
-                ],
-                axis=0,
-            )
-
-        def values(u, c):
-            n = lax.div(u, ROW) * ROW + 2 * c
+        def place(it, uu):
+            late = it >= stages - 2
+            stage = jnp.where(late, stages - 2 + uu, it)
+            g = jnp.where(late, it - (stages - 2), uu)
+            return stage, g
+
+        def scores(spot, c, h, upper):
+            stage, g = spot
+            keys = kv_in[pl.ds(stage * ROW + 2 * c, 2), 0:128, :].reshape(256, 128)
+            at = 0 if upper else HEAD
+            asking = jnp.concatenate(
+                [q_in[g * group + 2 * h + k, at : at + 128, :] for k in range(2)], axis=1
+            )
+            return jnp.dot(keys, asking, preferred_element_type=F32)
+
+        def values(spot, c):
+            n = spot[0] * ROW + 2 * c
             pieces = []
             for at in (128, 128 + HEAD):
                 for k in range(2):
@@ -281,76 +287,121 @@
                     )
             return jnp.concatenate(pieces, axis=1)
 
-        for g in range(ROW):
+        for g in range(2):
             high_s[g] = jnp.full((1, queries), -1e30, F32)
             total_s[g] = jnp.zeros((VROWS, queries), F32)
-        first = scores(0, 0)
-        score[0] = first
-
-        def body(u, top):
-            stage = lax.div(u, ROW)
-            g = lax.rem(u, ROW)
-
-            @pl.when((stage == 0) & (g < ROW - 1))
+
+        def ahead(slot, spot, c, h):
+            top = None
+            span = slice(h * strip, (h + 1) * strip)
+            for upper in range(2):
+                piece = scores(spot, c, h, upper)
+                score[slot, upper * 256 : (upper + 1) * 256, span] = piece
+                piece = jnp.max(piece, axis=0, keepdims=True)
+                top = piece if top is None else jnp.maximum(top, piece)
+            return top
+
+        def take(stage):
+            for k in range(ROW):
+                arrived(stage * ROW + k)
+                forward(stage * ROW + k).start()
+
+        def take_beside(stage):
+            for k in range(ROW):
+                forward(stage * ROW + k).wait_recv()
+
+        def body(it, top):
+            for uu in range(2):
+                spot = place(it, uu)
+                g = spot[1]
+                highest = high_s[g]
+                total = total_s[g]
+                for c in range(2):
+                    if c == 1 and uu == 0:
+
+                        @pl.when(it == stages - 2)
+                        def _():
+                            take_beside(ROW - 1)
+
+                    if c == 1 and uu == 1:
+
+                        @pl.when(it == 0)
+                        def _():
+                            for n in range(ROW, 3 * ROW):
+                                kv_copy(n).wait_send()
+                            for n in range(3 * ROW, PLANE):
+                                kv_copy(n).start()
+
+                        @pl.when(it < ROW - 1)
+                        def _():
+                            take(it + 1)
+
+                        @pl.when((it >= ROW - 1) & (it < stages - 2))
+                        def _():
+                            take_beside(it - (ROW - 1))
+
+                    if c == 0:
+                        after, c_after = spot, 1
+                    elif uu == 0:
+                        after, c_after = place(it, 1), 0
+                    else:
+                        after, c_after = place(jnp.minimum(it + 1, stages - 1), 0), 0
+                    raised = jnp.maximum(highest, top)
+                    fade = jnp.exp2(highest - raised)
+                    values_now = values(spot, c)
+                    tops, totals = [], []
+                    for h in range(queries // strip):
+                        span = slice(h * strip, (h + 1) * strip)
+                        piece = total[:, span] * fade[:, span]
+                        best = None
+                        for upper in range(2):
+                            rows = slice(upper * 256, (upper + 1) * 256)
+                            coming = scores(after, c_after, h, upper)
+                            weights = jnp.exp2(score[c, rows, span] - raised[:, span]).astype(BF16)
+                            score[1 - c, rows, span] = coming
+                            coming = jnp.max(coming, axis=0, keepdims=True)
+                            best = coming if best is None else jnp.maximum(best, coming)
+                            piece = piece + jnp.dot(
+                                values_now[:, rows], weights, preferred_element_type=F32
+                            )
+                        tops.append(best)
+                        totals.append(piece)
+                    top = jnp.concatenate(tops, axis=1)
+                    total = jnp.concatenate(totals, axis=1)
+                    highest = raised
+                high_s[g] = highest
+                total_s[g] = total
+
+            @pl.when(it >= stages - 2)
             def _():
-                for k in range(ROW):
-                    asked((g + 1) * ROW + k)
-
-            @pl.when((g == ROW - 1) & (stage < ROW - 1))
-            def _():
-                for k in range(ROW):
-                    n = (stage + 1) * ROW + k
-                    arrived(n)
-                    forward(n).start()
-
-            @pl.when((g == ROW - 1) & (stage >= ROW - 1) & (stage < stages - 1))
-            def _():
-                for k in range(ROW):
-                    forward((stage + 1 - ROW) * ROW + k).wait_recv()
-
-            highest = high_s[g]
-            total = total_s[g]
-            for slot in range(2):
-                raised = jnp.maximum(highest, top)
-                fade = jnp.exp2(highest - raised)
-                weights = jnp.exp2(score[slot] - raised).astype(BF16)
-                if slot == 0:
-                    ahead = scores(u, 1)
-                else:
-                    ahead = scores(jnp.minimum(u + 1, stages * ROW - 1), 0)
-                score[1 - slot] = ahead
-                top = jnp.max(ahead, axis=0, keepdims=True)
-                total = total * fade + jnp.dot(
-                    values(u, slot), weights, preferred_element_type=F32
-                )
-                highest = raised
-            high_s[g] = highest
-            total_s[g] = total
-
-            @pl.when(stage == stages - 1)
-            def _():
+                g = it - (stages - 2)
                 final = total_s[g]
                 mixed = (final[0:HEAD] / final[HEAD : HEAD + 1]).astype(BF16)
-                row_step = g + jnp.where(g == 2, 1, 0) - jnp.where(g == 3, 1, 0)
-                source_row = lax.rem(y + ROW - row_step, ROW)
-                for k in range(ROW):
-                    n = g * ROW + k
-                    o_out[n] = mixed[:, k * tokens : (k + 1) * tokens]
-                    source = source_row * ROW + lax.rem(x + ROW - k, ROW)
-                    back = remote(
-                        o_out.at[n], att.at[here], o_s.at[n], o_r.at[n], half * PLANE + source
-                    )
-                    if k == 0:
-
-                        @pl.when(g > 0)
-                        def _():
+                for r in range(2):
+                    row_step = jnp.where(g == 0, r, 3 - r)
+                    source_row = lax.rem(y + ROW - row_step, ROW)
+                    for k in range(ROW):
+                        n = g * group + r * ROW + k
+                        at = (r * ROW + k) * tokens
+                        o_out[n] = mixed[:, at : at + tokens]
+                        source = source_row * ROW + lax.rem(x + ROW - k, ROW)
+                        back = remote(
+                            o_out.at[n], att.at[here], o_s.at[n], o_r.at[n], half * PLANE + source
+                        )
+                        if r == 0 and k == 0:
+
+                            @pl.when(g > 0)
+                            def _():
+                                back.start()
+                        else:
                             back.start()
-                    else:
-                        back.start()
 
             return top
 
-        lax.fori_loop(0, stages * ROW, body, jnp.max(first, axis=0, keepdims=True))
+        top = jnp.concatenate(
+            [ahead(0, (0, 0), 0, h) for h in range(queries // strip)], axis=1
+        )
+        lax.fori_loop(0, stages, body, top)
         att[here] = o_out[0]
 
         def returned(n):
@@ -371,22 +422,27 @@
         loads[1].wait()
         loads[2].wait()
 
-        def mlp(c, total):
-            at = pl.multiple_of(c * step, step)
-            hidden = (
-                jnp.dot(normed_two, w1v[:, pl.ds(at, step)], preferred_element_type=F32)
-                + b1_ref[:, pl.ds(at, step)]
-            )
+        def expand(c):
+            span = slice(c * step, (c + 1) * step)
+            return (
+                jnp.dot(normed_two, w1v[:, span], preferred_element_type=F32) + b1_ref[:, span]
+            )
+
+        total = rows + b2_ref[...]
+        coming = expand(0)
+        for c in range(hidden_width // step):
+            hidden = coming
+            if c + 1 < hidden_width // step:
+                coming = expand(c + 1)
             hidden = 0.5 * hidden * (1.0 + lax.erf(hidden * math.sqrt(0.5)))
-            return total + jnp.dot(
-                hidden.astype(BF16), w2v[pl.ds(at, step), :], preferred_element_type=F32
-            )
-
-        out_ref[...] = lax.fori_loop(0, hidden_width // step, mlp, rows + b2_ref[...]).astype(BF16)
+            total = total + jnp.dot(
+                hidden.astype(BF16), w2v[c * step : (c + 1) * step, :], preferred_element_type=F32
+            )
+        out_ref[...] = total.astype(BF16)
         for n in range(1, PLANE):
-            q_copy(n).wait_send()
+            returned(n).wait_send()
+        for n in range(3 * ROW, PLANE):
             kv_copy(n).wait_send()
-            returned(n).wait_send()
         for n in range(PLANE):
             forward(n).wait_send()
 
@@ -419,8 +475,8 @@
             pltpu.VMEM((PLANE, 3 * HEAD, tokens), BF16),
             pltpu.VMEM((2 * PLANE, 256, 128), BF16),
             pltpu.VMEM((2, chunk, queries), F32),
-            pltpu.VMEM((ROW, 1, queries), F32),
-            pltpu.VMEM((ROW, VROWS, queries), F32),
+            pltpu.VMEM((2, 1, queries), F32),
+            pltpu.VMEM((2, VROWS, queries), F32),
             pltpu.VMEM((PLANE, HEAD, tokens), BF16),
             pltpu.VMEM((HEADS, HEAD, tokens), BF16),
             dma((count - 1,)), dma((count - 1,)), dma((2,)), dma((2,)),

time: 91.2 us -> 79.2 us (0.87); the launches traced: 89.7 us -> 78.8 us
  Pallas kernels: 87.8 us -> 76.9 us
    pallas_call x1, Pallas kernels: 87.8 us -> 76.9 us  [encoder(): pl.pallas_call(kernel, in_specs=[vmem, vmem, vmem, anywhere, vmem, vmem,...]
where the time goes in v2:
time: 79.2 us; the launch traced here: 78.8 us
  Pallas kernels  76.9 us (97%)
  local copies, waits for them, and re-layouts  1.87 us (2%)
    pallas_call x1, Pallas kernels, encoder(): pl.pallas_call(kernel, in_specs=[vmem, vmem, vmem, anywhere, vmem, vmem,...  76.9 us
    unnamed x1, local copies, waits for them, and re-layouts  1.87 us

profile of v2, /device:TPU:0, one launch (start us, length us, event | category | flops | bytes accessed | tf_op | source)
XLA Modules:
  0.0 78.8 jit_solution(5884482201468300679)
XLA Ops:
  0.0 76.9 %encoder.1 = bf16[256,1024]{1,0:T(8,128)(2,1)} custom-call(f32[4,64,64]{2,1,0:T(8,128)} %d_ref.1, bf16[216,1024]{1,0:T(8,128)(2,1)} %ws_ref.1, f32[1,1024]{1,0:T(1,128)} %bitcast.11, bf16[256,1024]{1,0:T(8,128)(2,1)} %pos_ref.1, f32[1,1024]{1,0:T(1,128)} %bitcast.12, f32[1,1024]{1,0:T(1,128)} %bitcast.13, bf16[1024,3072]{1,0:T(8,128)(2,1)} %wq_ref.1, ...), custom_call_target="tpu_custom_call" | custom-call | tf_op jit(solution)/shard_map/encoder/pallas_call | solution.py:452
  76.9 1.9 %copy.18 = bf16[256,1024]{1,0:T(8,128)(2,1)} copy(bf16[256,1024]{1,0:T(8,128)(2,1)} %encoder.1) | data formatting | bytes 1048576

commit v3 on v2

--- a/solution.py
+++ b/solution.py
@@ -72,9 +72,10 @@
     step = 512
 
     def kernel(
-        d_ref, ws_ref, sb_ref, pos_ref, g1_ref, s1_ref, wq_ref, qb_ref,
-        wo_ref, ob_ref, g2_ref, s2_ref, w1_ref, b1_ref, w2_ref, b2_ref,
+        d_hbm, ws_hbm, sb_hbm, pos_ref, g1_hbm, s1_hbm, wq_ref, qb_hbm,
+        wo_ref, ob_hbm, g2_hbm, s2_hbm, w1_ref, b1_hbm, w2_ref, b2_hbm,
         out_ref,
+        d_ref, ws_ref, sb_ref, g1_ref, s1_ref, qb_ref, ob_ref, g2_ref, s2_ref, b1_ref, b2_ref,
         mine, sums, halo, fp, x6, w6, wq, posv, wo, w1v, w2v, resv,
         q_out, kv_out, q_in, kv_in, score, high_s, total_s, o_out, att,
         sum_s, sum_r, halo_s, halo_r, q_s, q_r, kv_s, kv_r, f_s, f_r, o_s, o_r, load,
@@ -87,10 +88,23 @@
         peers = [lax.rem(me + i, count) for i in range(1, count)]
         barrier = greet(peers)
         load_w = pltpu.make_async_copy(wq_ref, wq, load.at[0])
+        load_p = pltpu.make_async_copy(pos_ref, posv, load.at[1])
+
+        small = [
+            pltpu.make_async_copy(source, target, load.at[5 + i])
+            for i, (source, target) in enumerate(
+                (
+                    (d_hbm, d_ref), (ws_hbm, ws_ref), (sb_hbm, sb_ref), (g1_hbm, g1_ref),
+                    (s1_hbm, s1_ref), (qb_hbm, qb_ref), (ob_hbm, ob_ref), (g2_hbm, g2_ref),
+                    (s2_hbm, s2_ref), (b1_hbm, b1_ref), (b2_hbm, b2_ref),
+                )
+            )
+        ]
+        for copy in small:
+            copy.start()
         load_w.start()
-        load_p = pltpu.make_async_copy(pos_ref, posv, load.at[1])
         load_p.start()
-
+        small[0].wait()
         slab = d_ref[...]
         part = jnp.sum(slab, axis=0)
         part = jnp.sum(part, axis=0, keepdims=True)
@@ -98,6 +112,8 @@
         mine[...] = jnp.broadcast_to(part, (8, 128))
         fp[...] = jnp.zeros(fp.shape, F32)
         w6[...] = jnp.zeros(w6.shape, BF16)
+        for copy in small[1:]:
+            copy.wait()
         for a in range(6):
             w6[a * 128 : a * 128 + 36, :] = ws_ref[a * 36 : (a + 1) * 36, :]
         pl.semaphore_wait(barrier, count - 1)
@@ -219,19 +235,26 @@
             head = order[n][2] * ROW + order[n][3]
             return remote(kv_out.at[head], kv_in.at[n], kv_s.at[n], kv_r.at[n], half * PLANE + head)
 
-        make_kv(order[0][2])
-        kv_in[0] = kv_out[here]
-        for n in range(1, ROW):
-            kv_copy(n).start()
-        remote(kv_out.at[here], kv_in.at[PLANE], f_s.at[0], f_r.at[0], beside).start()
-        for g in range(ROW):
+        def send_kv(g):
+            make_kv(order[g * ROW][2])
+            for n in range(g * ROW, (g + 1) * ROW):
+                if n:
+                    kv_copy(n).start()
+
+        def send_q(g):
             make_q(order[g * ROW][2])
             for n in range(g * ROW, (g + 1) * ROW):
                 if n:
                     q_copy(n).start()
+
+        send_kv(0)
+        remote(kv_out.at[here], kv_in.at[PLANE], f_s.at[0], f_r.at[0], beside).start()
+        for g in range(ROW):
+            send_q(g)
+        for g in range(1, ROW):
+            send_kv(g)
+        kv_in[0] = kv_out[here]
         q_in[0, HEAD : 2 * HEAD, :] = q_out[here]
-        for g in range(1, ROW):
-            make_kv(order[g * ROW][2])
 
         def forward(n):
             return remote(kv_in.at[n], kv_in.at[PLANE + n], f_s.at[n], f_r.at[n], beside)
@@ -247,26 +270,14 @@
         for n in range(1, ROW):
             arrived(n)
             forward(n).start()
-        for n in range(1, ROW):
-            kv_copy(n).wait_send()
-        for n in range(1, PLANE):
-            q_copy(n).wait_send()
-        for n in range(ROW, 3 * ROW):
-            kv_copy(n).start()
+        for n in range(1, group):
+            asked(n)
         for copy in loads:
             copy.start()
-        for n in range(1, PLANE):
-            asked(n)
 
         ones = jnp.where(
             lax.broadcasted_iota(jnp.int32, (VROWS - HEAD, 128), 0) == 0, 1.0, 0.0
         ).astype(BF16)
-
-        def place(it, uu):
-            late = it >= stages - 2
-            stage = jnp.where(late, stages - 2 + uu, it)
-            g = jnp.where(late, it - (stages - 2), uu)
-            return stage, g
 
         def scores(spot, c, h, upper):
             stage, g = spot
@@ -310,98 +321,91 @@
             for k in range(ROW):
                 forward(stage * ROW + k).wait_recv()
 
+        def advance(spot, c, after, c_after, highest, total, top, finish=None):
+            raised = jnp.maximum(highest, top)
+            fade = jnp.exp2(highest - raised)
+            values_now = values(spot, c)
+            tops, totals = [], []
+            for h in range(queries // strip):
+                span = slice(h * strip, (h + 1) * strip)
+                piece = total[:, span] * fade[:, span]
+                best = None
+                for upper in range(2):
+                    rows = slice(upper * 256, (upper + 1) * 256)
+                    if after is not None:
+                        coming = scores(after, c_after, h, upper)
+                    weights = jnp.exp2(score[c, rows, span] - raised[:, span]).astype(BF16)
+                    if after is not None:
+                        score[1 - c, rows, span] = coming
+                        coming = jnp.max(coming, axis=0, keepdims=True)
+                        best = coming if best is None else jnp.maximum(best, coming)
+                    piece = piece + jnp.dot(
+                        values_now[:, rows], weights, preferred_element_type=F32
+                    )
+                tops.append(best)
+                totals.append(piece)
+                if finish is not None:
+                    finish(spot[1], h, piece)
+            if after is not None:
+                top = jnp.concatenate(tops, axis=1)
+            return raised, jnp.concatenate(totals, axis=1), top
+
         def body(it, top):
-            for uu in range(2):
-                spot = place(it, uu)
-                g = spot[1]
-                highest = high_s[g]
-                total = total_s[g]
-                for c in range(2):
-                    if c == 1 and uu == 0:
-
-                        @pl.when(it == stages - 2)
-                        def _():
-                            take_beside(ROW - 1)
-
-                    if c == 1 and uu == 1:
-
-                        @pl.when(it == 0)
-                        def _():
-                            for n in range(ROW, 3 * ROW):
-                                kv_copy(n).wait_send()
-                            for n in range(3 * ROW, PLANE):
-                                kv_copy(n).start()
-
-                        @pl.when(it < ROW - 1)
-                        def _():
-                            take(it + 1)
-
-                        @pl.when((it >= ROW - 1) & (it < stages - 2))
-                        def _():
-                            take_beside(it - (ROW - 1))
-
-                    if c == 0:
-                        after, c_after = spot, 1
-                    elif uu == 0:
-                        after, c_after = place(it, 1), 0
-                    else:
-                        after, c_after = place(jnp.minimum(it + 1, stages - 1), 0), 0
-                    raised = jnp.maximum(highest, top)
-                    fade = jnp.exp2(highest - raised)
-                    values_now = values(spot, c)
-                    tops, totals = [], []
-                    for h in range(queries // strip):
-                        span = slice(h * strip, (h + 1) * strip)
-                        piece = total[:, span] * fade[:, span]
-                        best = None
-                        for upper in range(2):
-                            rows = slice(upper * 256, (upper + 1) * 256)
-                            coming = scores(after, c_after, h, upper)
-                            weights = jnp.exp2(score[c, rows, span] - raised[:, span]).astype(BF16)
-                            score[1 - c, rows, span] = coming
-                            coming = jnp.max(coming, axis=0, keepdims=True)
-                            best = coming if best is None else jnp.maximum(best, coming)
-                            piece = piece + jnp.dot(
-                                values_now[:, rows], weights, preferred_element_type=F32
-                            )
-                        tops.append(best)
-                        totals.append(piece)
-                    top = jnp.concatenate(tops, axis=1)
-                    total = jnp.concatenate(totals, axis=1)
-                    highest = raised
+            for g in range(2):
+                highest, total = high_s[g], total_s[g]
+                highest, total, top = advance((it, g), 0, (it, g), 1, highest, total, top)
+                if g == 1:
+
+                    @pl.when(it < ROW - 1)
+                    def _():
+                        take(it + 1)
+
+                    @pl.when(it >= ROW - 1)
+                    def _():
+                        take_beside(it - (ROW - 1))
+
+                after = (it, 1) if g == 0 else (it + 1, 0)
+                highest, total, top = advance((it, g), 1, after, 0, highest, total, top)
                 high_s[g] = highest
                 total_s[g] = total
-
-            @pl.when(it >= stages - 2)
-            def _():
-                g = it - (stages - 2)
-                final = total_s[g]
-                mixed = (final[0:HEAD] / final[HEAD : HEAD + 1]).astype(BF16)
-                for r in range(2):
-                    row_step = jnp.where(g == 0, r, 3 - r)
-                    source_row = lax.rem(y + ROW - row_step, ROW)
-                    for k in range(ROW):
-                        n = g * group + r * ROW + k
-                        at = (r * ROW + k) * tokens
-                        o_out[n] = mixed[:, at : at + tokens]
-                        source = source_row * ROW + lax.rem(x + ROW - k, ROW)
-                        back = remote(
-                            o_out.at[n], att.at[here], o_s.at[n], o_r.at[n], half * PLANE + source
-                        )
-                        if r == 0 and k == 0:
-
-                            @pl.when(g > 0)
-                            def _():
-                                back.start()
-                        else:
-                            back.start()
-
             return top
+
+        def finish(g, h, piece):
+            mixed = (piece[0:HEAD] / piece[HEAD : HEAD + 1]).astype(BF16)
+            for k in range(2):
+                n = g * group + 2 * h + k
+                o_out[n] = mixed[:, k * tokens : (k + 1) * tokens]
+                if n:
+                    i, j = order[n][0], order[n][1]
+                    source = lax.rem(y + ROW - i, ROW) * ROW + lax.rem(x + ROW - j, ROW)
+                    remote(
+                        o_out.at[n], att.at[here], o_s.at[n], o_r.at[n], half * PLANE + source
+                    ).start()
 
         top = jnp.concatenate(
             [ahead(0, (0, 0), 0, h) for h in range(queries // strip)], axis=1
         )
-        lax.fori_loop(0, stages, body, top)
+        for g in range(2):
+            highest, total, top = advance((0, g), 0, (0, g), 1, high_s[g], total_s[g], top)
+            if g == 0:
+                for n in range(group, PLANE):
+                    asked(n)
+            else:
+                take(1)
+            after = (0, 1) if g == 0 else (1, 0)
+            highest, total, top = advance((0, g), 1, after, 0, highest, total, top)
+            high_s[g] = highest
+            total_s[g] = total
+        top = lax.fori_loop(1, stages - 1, body, top)
+        last = stages - 1
+        for g in range(2):
+            highest, total, top = advance(
+                (last, g), 0, (last, g), 1, high_s[g], total_s[g], top
+            )
+            after = (last, 1) if g == 0 else None
+            highest, total, top = advance(
+                (last, g), 1, after, 0, highest, total, top, finish
+            )
         att[here] = o_out[0]
 
         def returned(n):
@@ -441,8 +445,9 @@
         out_ref[...] = total.astype(BF16)
         for n in range(1, PLANE):
             returned(n).wait_send()
-        for n in range(3 * ROW, PLANE):
+        for n in range(1, PLANE):
             kv_copy(n).wait_send()
+            q_copy(n).wait_send()
         for n in range(PLANE):
             forward(n).wait_send()
 
@@ -451,13 +456,21 @@
     dma = pltpu.SemaphoreType.DMA
     return pl.pallas_call(
         kernel,
-        in_specs=[
-            vmem, vmem, vmem, anywhere, vmem, vmem, anywhere, vmem,
-            anywhere, vmem, vmem, vmem, anywhere, vmem, anywhere, vmem,
-        ],
+        in_specs=[anywhere] * 16,
         out_specs=vmem,
         out_shape=jax.ShapeDtypeStruct((tokens, width), BF16),
         scratch_shapes=[
+            pltpu.VMEM(density.shape, F32),
+            pltpu.VMEM(stem_weight.shape, BF16),
+            pltpu.VMEM(stem_bias.shape, F32),
+            pltpu.VMEM(gain1.shape, F32),
+            pltpu.VMEM(shift1.shape, F32),
+            pltpu.VMEM(qkv_bias.shape, F32),
+            pltpu.VMEM(out_bias.shape, F32),
+            pltpu.VMEM(gain2.shape, F32),
+            pltpu.VMEM(shift2.shape, F32),
+            pltpu.VMEM(b1.shape, F32),
+            pltpu.VMEM(b2.shape, F32),
             pltpu.VMEM((8, 128), F32),
             pltpu.VMEM((count - 1, 8, 128), F32),
             pltpu.VMEM((2, side, side), F32),
@@ -481,7 +494,7 @@
             pltpu.VMEM((HEADS, HEAD, tokens), BF16),
             dma((count - 1,)), dma((count - 1,)), dma((2,)), dma((2,)),
             dma((PLANE,)), dma((PLANE,)), dma((PLANE,)), dma((PLANE,)),
-            dma((PLANE,)), dma((PLANE,)), dma((PLANE,)), dma((PLANE,)), dma((5,)),
+            dma((PLANE,)), dma((PLANE,)), dma((PLANE,)), dma((PLANE,)), dma((16,)),
         ],
         compiler_params=pltpu.CompilerParams(
             vmem_limit_bytes=VMEM_LIMIT, collective_id=0, has_side_effects=True

time: 79.2 us -> 73.3 us (0.926)
  Pallas kernels: 76.9 us -> 70.7 us
    pallas_call x1, Pallas kernels: 76.9 us -> 70.7 us  [encoder(): pl.pallas_call(kernel, in_specs=[anywhere] * 16, out_specs=vmem, out_shap...]
where the time goes in v3:
time: 73.3 us; the launch traced here: 72.6 us
  Pallas kernels  70.7 us (96%)
  local copies, waits for them, and re-layouts  1.87 us (3%)
    pallas_call x1, Pallas kernels, encoder(): pl.pallas_call(kernel, in_specs=[anywhere] * 16, out_specs=vmem, out_shap...  70.7 us
    unnamed x1, local copies, waits for them, and re-layouts  1.87 us

profile of v3, /device:TPU:0, one launch (start us, length us, event | category | flops | bytes accessed | tf_op | source)
XLA Modules:
  0.0 72.6 jit_solution(12653006584924236490)
XLA Ops:
  0.0 70.7 %encoder.1 = bf16[256,1024]{1,0:T(8,128)(2,1)} custom-call(f32[4,64,64]{2,1,0:T(8,128)} %d_hbm.1, bf16[216,1024]{1,0:T(8,128)(2,1)} %ws_hbm.1, f32[1,1024]{1,0:T(1,128)} %bitcast.11, bf16[256,1024]{1,0:T(8,128)(2,1)} %pos_ref.1, f32[1,1024]{1,0:T(1,128)} %bitcast.12, f32[1,1024]{1,0:T(1,128)} %bitcast.13, bf16[1024,3072]{1,0:T(8,128)(2,1)} %wq_ref.1, ...), custom_call_target="tpu_custom_call" | custom-call | tf_op jit(solution)/shard_map/encoder/pallas_call | solution.py:457
  70.7 1.9 %copy.18 = bf16[256,1024]{1,0:T(8,128)(2,1)} copy(bf16[256,1024]{1,0:T(8,128)(2,1)} %encoder.1) | data formatting | bytes 1048576

commit v4 on v3

--- a/solution.py
+++ b/solution.py
@@ -76,7 +76,7 @@
         wo_ref, ob_hbm, g2_hbm, s2_hbm, w1_ref, b1_hbm, w2_ref, b2_hbm,
         out_ref,
         d_ref, ws_ref, sb_ref, g1_ref, s1_ref, qb_ref, ob_ref, g2_ref, s2_ref, b1_ref, b2_ref,
-        mine, sums, halo, fp, x6, w6, wq, posv, wo, w1v, w2v, resv,
+        mine, sums, halo, fp, picks, turned_at, x6, w6, wq, posv, wo, w1v, w2v, resv,
         q_out, kv_out, q_in, kv_in, score, high_s, total_s, o_out, att,
         sum_s, sum_r, halo_s, halo_r, q_s, q_r, kv_s, kv_r, f_s, f_r, o_s, o_r, load,
     ):
@@ -109,7 +109,7 @@
         part = jnp.sum(slab, axis=0)
         part = jnp.sum(part, axis=0, keepdims=True)
         part = jnp.sum(part, axis=1, keepdims=True)
-        mine[...] = jnp.broadcast_to(part, (8, 128))
+        mine[...] = jnp.broadcast_to(part, (1, 128))
         fp[...] = jnp.zeros(fp.shape, F32)
         w6[...] = jnp.zeros(w6.shape, BF16)
         for copy in small[1:]:
@@ -130,6 +130,19 @@
         for i in range(PLANE):
             q_in[i, 0:HEAD, :] = jnp.zeros((HEAD, tokens), BF16)
             q_in[i, 2 * HEAD : 3 * HEAD, :] = jnp.zeros((HEAD, tokens), BF16)
+        z = lax.broadcasted_iota(jnp.int32, (side, lanes), 0)
+        col = lax.broadcasted_iota(jnp.int32, (side, lanes), 1)
+        lane = jnp.bitwise_and(col, 127)
+        base = z + 1 - 4 * jnp.right_shift(col, 7) - lane
+        for b in range(6):
+            pick = (base == -6 * b) & (lane >= 6 * b) & (lane < 6 * b + 6)
+            picks[b] = jnp.where(pick, 1.0, 0.0).astype(BF16)
+        r = lax.broadcasted_iota(jnp.int32, (tokens, tokens), 0)
+        s = lax.broadcasted_iota(jnp.int32, (tokens, tokens), 1)
+        turn = (jnp.right_shift(r, 4) == jnp.bitwise_and(s, 15)) & (
+            jnp.bitwise_and(r, 15) == jnp.right_shift(s, 4)
+        )
+        turned_at[...] = jnp.where(turn, 1.0, 0.0).astype(BF16)
         for share in shares:
             share.wait()
         to_up.wait()
@@ -150,34 +163,20 @@
         at = (planes + 1) * pad + 1
         fp[at : at + side, 0:side] = high
 
-        z = lax.broadcasted_iota(jnp.int32, (side, lanes), 0)
-        col = lax.broadcasted_iota(jnp.int32, (side, lanes), 1)
-        lane = jnp.bitwise_and(col, 127)
-        base = z + 1 - 4 * jnp.right_shift(col, 7) - lane
         spread = jnp.zeros((6 * grid, lanes), F32)
         for b in range(6):
             rows = jnp.concatenate(
                 [fp[pl.ds(a * pad + b, grid, stride=4), 0:side] for a in range(6)], axis=0
             )
-            pick = (base == -6 * b) & (lane >= 6 * b) & (lane < 6 * b + 6)
-            spread += jnp.dot(
-                rows.astype(BF16),
-                jnp.where(pick, 1.0, 0.0).astype(BF16),
-                preferred_element_type=F32,
-            )
+            spread += jnp.dot(rows.astype(BF16), picks[b], preferred_element_type=F32)
         spread = spread.astype(BF16)
         for k in range(grid):
             for a in range(6):
                 x6[k * grid : (k + 1) * grid, a * 128 : (a + 1) * 128] = spread[
                     a * grid : (a + 1) * grid, k * 128 : (k + 1) * 128
                 ]
-        r = lax.broadcasted_iota(jnp.int32, (tokens, tokens), 0)
-        s = lax.broadcasted_iota(jnp.int32, (tokens, tokens), 1)
-        turn = (jnp.right_shift(r, 4) == jnp.bitwise_and(s, 15)) & (
-            jnp.bitwise_and(r, 15) == jnp.right_shift(s, 4)
-        )
         patches = jnp.dot(
-            jnp.where(turn, 1.0, 0.0).astype(BF16), x6[...], preferred_element_type=F32
+            turned_at[...], x6[...], preferred_element_type=F32
         ).astype(BF16)
         load_p.wait()
         embedded = (
@@ -206,13 +205,13 @@
             )
 
         def make_q(row):
-            turned = (project(0, row) * scale).T.astype(BF16)
+            turned = (project(0, row) * scale).astype(BF16).T
             for k in range(ROW):
                 q_out[row * ROW + k] = turned[k * HEAD : (k + 1) * HEAD, :]
 
         def make_kv(row):
             keys = project(1, row)
-            turned = project(2, row).T.astype(BF16)
+            turned = project(2, row).astype(BF16).T
             for k in range(ROW):
                 pair = keys[:, (k // 2) * 128 : (k // 2 + 1) * 128]
                 lo, hi = pair[0:128], pair[128:256]
@@ -350,22 +349,26 @@
                 top = jnp.concatenate(tops, axis=1)
             return raised, jnp.concatenate(totals, axis=1), top
 
+        def stage_at(it):
+            return jnp.where(it == 1, ROW, jnp.where(it <= ROW, it - 1, it))
+
         def body(it, top):
+            stage, coming_stage = stage_at(it), stage_at(it + 1)
             for g in range(2):
                 highest, total = high_s[g], total_s[g]
-                highest, total, top = advance((it, g), 0, (it, g), 1, highest, total, top)
+                highest, total, top = advance((stage, g), 0, (stage, g), 1, highest, total, top)
                 if g == 1:
 
-                    @pl.when(it < ROW - 1)
+                    @pl.when(it < ROW)
                     def _():
-                        take(it + 1)
-
-                    @pl.when(it >= ROW - 1)
+                        take(it)
+
+                    @pl.when(it >= ROW)
                     def _():
                         take_beside(it - (ROW - 1))
 
-                after = (it, 1) if g == 0 else (it + 1, 0)
-                highest, total, top = advance((it, g), 1, after, 0, highest, total, top)
+                after = (stage, 1) if g == 0 else (coming_stage, 0)
+                highest, total, top = advance((stage, g), 1, after, 0, highest, total, top)
                 high_s[g] = highest
                 total_s[g] = total
             return top
@@ -391,8 +394,8 @@
                 for n in range(group, PLANE):
                     asked(n)
             else:
-                take(1)
-            after = (0, 1) if g == 0 else (1, 0)
+                take_beside(0)
+            after = (0, 1) if g == 0 else (ROW, 0)
             highest, total, top = advance((0, g), 1, after, 0, highest, total, top)
             high_s[g] = highest
             total_s[g] = total
@@ -412,15 +415,19 @@
             head = order[n][2] * ROW + order[n][3]
             return remote(o_out.at[n], att.at[head], o_s.at[n], o_r.at[n], beside)
 
-        for n in range(1, PLANE):
-            returned(n).wait_recv()
         loads[0].wait()
-        attended = att[...].reshape(width, tokens).T
-        stream = (
-            resv[...].astype(F32)
-            + jnp.dot(attended, wo[...], preferred_element_type=F32)
-            + ob_ref[...]
-        ).astype(BF16)
+        summed = resv[...].astype(F32) + ob_ref[...]
+        for g in range(ROW):
+            for n in range(g * ROW, (g + 1) * ROW):
+                if n:
+                    returned(n).wait_recv()
+            row = order[g * ROW][2]
+            attended = att[pl.ds(row * ROW, ROW)].reshape(ROW * HEAD, tokens).T
+            at = pl.multiple_of(row * ROW * HEAD, ROW * HEAD)
+            summed = summed + jnp.dot(
+                attended, wo[pl.ds(at, ROW * HEAD), :], preferred_element_type=F32
+            )
+        stream = summed.astype(BF16)
         rows = stream.astype(F32)
         normed_two = normalize(rows, g2_ref[...], s2_ref[...]).astype(BF16)
         loads[1].wait()
@@ -471,10 +478,12 @@
             pltpu.VMEM(shift2.shape, F32),
             pltpu.VMEM(b1.shape, F32),
             pltpu.VMEM(b2.shape, F32),
-            pltpu.VMEM((8, 128), F32),
-            pltpu.VMEM((count - 1, 8, 128), F32),
+            pltpu.VMEM((1, 128), F32),
+            pltpu.VMEM((count - 1, 1, 128), F32),
             pltpu.VMEM((2, side, side), F32),
             pltpu.VMEM((6 * pad, 128), F32),
+            pltpu.VMEM((6, side, lanes), BF16),
+            pltpu.VMEM((tokens, tokens), BF16),
             pltpu.VMEM((tokens, 6 * 128), BF16),
             pltpu.VMEM((6 * 128, width), BF16),
             pltpu.VMEM(w_qkv.shape, BF16),

time: 73.3 us -> 70.6 us (0.963)
  Pallas kernels: 70.7 us -> 68.6 us
    pallas_call x1, Pallas kernels: 70.7 us -> 68.6 us  [encoder(): pl.pallas_call(kernel, in_specs=[anywhere] * 16, out_specs=vmem, out_shap...]
where the time goes in v4:
time: 70.6 us; the launch traced here: 70.4 us
  Pallas kernels  68.6 us (97%)
  local copies, waits for them, and re-layouts  1.87 us (3%)
    pallas_call x1, Pallas kernels, encoder(): pl.pallas_call(kernel, in_specs=[anywhere] * 16, out_specs=vmem, out_shap...  68.6 us
    unnamed x1, local copies, waits for them, and re-layouts  1.87 us

profile of v4, /device:TPU:0, one launch (start us, length us, event | category | flops | bytes accessed | tf_op | source)
XLA Modules:
  0.0 70.4 jit_solution(1537844516808441524)
XLA Ops:
  0.0 68.6 %encoder.1 = bf16[256,1024]{1,0:T(8,128)(2,1)} custom-call(f32[4,64,64]{2,1,0:T(8,128)} %d_hbm.1, bf16[216,1024]{1,0:T(8,128)(2,1)} %ws_hbm.1, f32[1,1024]{1,0:T(1,128)} %bitcast.11, bf16[256,1024]{1,0:T(8,128)(2,1)} %pos_ref.1, f32[1,1024]{1,0:T(1,128)} %bitcast.12, f32[1,1024]{1,0:T(1,128)} %bitcast.13, bf16[1024,3072]{1,0:T(8,128)(2,1)} %wq_ref.1, ...), custom_call_target="tpu_custom_call" | custom-call | tf_op jit(solution)/shard_map/encoder/pallas_call | solution.py:464
  68.6 1.9 %copy.18 = bf16[256,1024]{1,0:T(8,128)(2,1)} copy(bf16[256,1024]{1,0:T(8,128)(2,1)} %encoder.1) | data formatting | bytes 1048576
